TPU v7x, 128 devices: a whole 4x4x4 slice. The times are simulated.
128 devices in a mesh: dp: 16 (over y, x), mp: 8 (over z, core).
Axes of the slice: x: 4, y: 4, z: 4, core: 2. Of those that a mesh axis runs over, the one named last changes fastest.
Arguments:
- tokens: bfloat16 [65536, 1024], P(('dp', 'mp')), may hold values from -6 to 6
- norm_gain: float32 [2, 1024], replicated, may hold values from 0.1 to 1.9
- qkv_weight: bfloat16 [3, 1024, 1024], P(None, 'dp', 'mp')
- out_weight: bfloat16 [1024, 1024], P('mp', 'dp'), may hold values from -0.1875 to 0.1875
- variate_bias: float32 [2, 16], replicated, may hold values from -6 to 6
- ffn_weight: bfloat16 [2, 1024, 2816], P(None, 'dp', 'mp'), may hold values from -0.1875 to 0.1875
- down_weight: bfloat16 [2816, 1024], P('mp', 'dp'), may hold values from -0.109375 to 0.109375
- sample_ids: int32 [65536], P(('dp', 'mp')), may hold values from 0 to 127, as said below
- variate_ids: int32 [65536], P(('dp', 'mp')), may hold values from 0 to 15, as said below
- time_ids: int32 [65536], P(('dp', 'mp')), may hold values from 0 to 31, as said below
Outputs:
- encoded: bfloat16 [65536, 1024], P(('dp', 'mp'))
Inputs may be any that keep to these rules, and one draw needn't show every extreme that they name: `sample_ids`: within each packed sequence of 512 tokens the series numbers start at 0 and never fall; a series with v variates (1 to 16) and p patches (4 to 32) holds v * p consecutive tokens, the last series of a sequence may be cut short; some packed sequence holds 128 series of one variate and four patches each. `variate_ids`: A token's offset within its series divided by that series' patch count p. `time_ids`: A token's offset within its series modulo that series' patch count p.
All inputs are finite; a program needn't handle non-finite values.
Results may differ from a plain program's by a relative error of at most 0.017.
Values may be sent and summed in bfloat16 or wider, within the bound.
A program may use at most 128 MiB of HBM per device.

v0:
```python
import jax
import jax.numpy as jnp
from jax import lax
from jax.sharding import PartitionSpec as P

HEAD_DIM = 64
L = 512


def sent_to_all(shard, axis):
    copies = jnp.broadcast_to(shard, (lax.axis_size(axis), *shard.shape))
    return lax.all_to_all(copies, axis, split_axis=0, concat_axis=0, tiled=True)


def in_order(blocks, dim):
    blocks = jnp.moveaxis(blocks, 0, dim)
    dims = blocks.shape
    return blocks.reshape(*dims[:dim], dims[dim] * dims[dim + 1], *dims[dim + 2 :])


def collect(shard, axis, dim):
    blocks = sent_to_all(shard, axis)
    return in_order(blocks, dim)


def rows_first(arrays, axis, dims):
    turned = [jnp.moveaxis(a, dim, 0) for a, dim in zip(arrays, dims)]
    widths = [t[0].size for t in turned]
    both = jnp.concatenate([t.reshape(-1, w) for t, w in zip(turned, widths)], axis=1)
    whole = lax.all_gather(both, axis, axis=0, tiled=True)
    blocks = jnp.split(whole, [sum(widths[:k]) for k in range(1, len(widths))], axis=1)
    return tuple(
        (
            jnp.moveaxis(b.reshape(-1, *t.shape[1:]), 0, dim)
            for b, t, dim in zip(blocks, turned, dims)
        )
    )


def rms_norm(values, gain):
    wide = values.astype(jnp.float32)
    square = jnp.mean(wide * wide, axis=-1, keepdims=True)
    return (wide * lax.rsqrt(square + 1e-05) * gain[None, :]).astype(jnp.bfloat16)


def rotate(values, times):
    half = values.shape[-1] // 2
    freq = 10000.0 ** (-jnp.arange(half, dtype=jnp.float32) / half)
    angle = times.astype(jnp.float32)[:, None] * freq[None, :]
    cosine = jnp.cos(angle)[:, None, :]
    sine = jnp.sin(angle)[:, None, :]
    first = values[..., :half]
    second = values[..., half:]
    return jnp.concatenate(
        [first * cosine - second * sine, first * sine + second * cosine], axis=-1
    )


def rotated(raw, times):
    row_total, local_width = raw.shape
    turned = rotate(raw.reshape(row_total, local_width // HEAD_DIM, HEAD_DIM), times)
    return turned.reshape(row_total, local_width).astype(jnp.bfloat16)


def attend(queries, keys_rot, values, samples, variates, bias):
    row_total, local_width = queries.shape
    heads_here = local_width // HEAD_DIM
    count = row_total // L

    def one_sequence(args):
        qs, ks, vs, sample_row, variate_row = args
        scores = jnp.einsum(
            "qhd,khd->hqk", qs, ks, preferred_element_type=jnp.float32
        ) * HEAD_DIM ** (-0.5)
        same = variate_row[:, None] == variate_row[None, :]
        scores = scores + jnp.where(same[None], bias[0][:, None, None], bias[1][:, None, None])
        scores = jnp.where((sample_row[:, None] == sample_row[None, :])[None], scores, -1e30)
        top = jnp.max(scores, axis=2, keepdims=True)
        expo = jnp.exp(scores - top)
        weights = (expo / jnp.sum(expo, axis=2, keepdims=True)).astype(jnp.bfloat16)
        return jnp.einsum("hqk,khd->qhd", weights, vs, preferred_element_type=jnp.float32).astype(
            jnp.bfloat16
        )

    shape = (count, L, heads_here, HEAD_DIM)
    result = lax.map(
        one_sequence,
        (
            queries.reshape(shape),
            keys_rot.reshape(shape),
            values.reshape(shape),
            samples.reshape(count, L),
            variates.reshape(count, L),
        ),
    )
    return result.reshape(row_total, local_width)


def local(
    tokens,
    norm_gain,
    qkv_weight,
    out_weight,
    variate_bias,
    ffn_weight,
    down_weight,
    sample_ids,
    variate_ids,
    time_ids,
):
    heads_here = qkv_weight.shape[2] // HEAD_DIM
    head_start = lax.axis_index("mp") * heads_here
    bias_local = lax.dynamic_slice_in_dim(variate_bias, head_start, heads_here, 1)
    first_normed = rms_norm(tokens, norm_gain[0])
    wide_columns = collect(qkv_weight, "mp", 2)
    columns = first_normed
    projected = jnp.einsum(
        "rc,jcd->jrd",
        columns,
        lax.all_gather(wide_columns, "dp", axis=1, tiled=True),
        preferred_element_type=jnp.float32,
    )
    queries = rotated(projected[0], time_ids)
    keys_rot = rotated(projected[1], time_ids)
    values = projected[2].astype(jnp.bfloat16)
    grouped = lax.all_to_all(
        jnp.stack([queries, keys_rot, values]), "mp", split_axis=2, concat_axis=1, tiled=True
    )
    gathered_ids = rows_first((sample_ids, variate_ids), "mp", (0, 0))
    attended = attend(
        grouped[0], grouped[1], grouped[2], gathered_ids[0], gathered_ids[1], bias_local
    )
    back_rows = lax.all_to_all(attended, "mp", split_axis=0, concat_axis=1, tiled=True)
    out_rows = collect(out_weight, "mp", 0)
    mixed = jnp.dot(back_rows, collect(out_rows, "dp", 1), preferred_element_type=jnp.float32)
    residual = (tokens.astype(jnp.float32) + mixed).astype(jnp.bfloat16)
    second_normed = rms_norm(residual, norm_gain[1])
    ffn_columns = collect(ffn_weight, "mp", 2)
    columns = second_normed
    gate_up = jnp.einsum(
        "rc,jcf->jrf",
        columns,
        lax.all_gather(ffn_columns, "dp", axis=1, tiled=True),
        preferred_element_type=jnp.float32,
    )
    hidden = (jax.nn.silu(gate_up[0]) * gate_up[1]).astype(jnp.bfloat16)
    down_full = collect(down_weight, "mp", 0)
    feed = jnp.dot(
        hidden,
        lax.all_gather(down_full, "dp", axis=1, tiled=True),
        preferred_element_type=jnp.float32,
    )
    return (residual.astype(jnp.float32) + feed).astype(jnp.bfloat16)


def solution(mesh):
    return jax.shard_map(
        local,
        mesh=mesh,
        in_specs=(
            P(("dp", "mp"), None),
            P(),
            P(None, "dp", "mp"),
            P("mp", "dp"),
            P(),
            P(None, "dp", "mp"),
            P("mp", "dp"),
            P(("dp", "mp")),
            P(("dp", "mp")),
            P(("dp", "mp")),
        ),
        out_specs=P(("dp", "mp"), None),
        check_vma=False,
    )
```

profile of v0, /device:TPU:2, one launch (start us, length us, event | category | flops | bytes accessed | tf_op | source)
XLA Modules:
  0.0 293.8 jit_solution(12576738158072073453)
XLA Ops:
  7.5 14.0 %all_to_all.59 = bf16[8,3,64,128]{3,2,1,0:T(8,128)(2,1)S(1)} all-to-all(bf16[8,3,64,128]{3,2,1,0:T(8,128)(2,1)S(1)} %broadcast_in_dim.81), channel_id=1, replica_groups=mesh['dp'=16,'mp'=8] {'mp'}, dimensions={0} | all-to-all | bytes 786432 | tf_op jit(solution)/shard_map/all_to_all | solution.py:12
  22.5 15.6 %all_to_all.60 = bf16[8,2,64,352]{3,2,1,0:T(8,128)(2,1)S(1)} all-to-all(bf16[8,2,64,352]{3,2,1,0:T(8,128)(2,1)S(1)} %broadcast_in_dim.84), channel_id=1, replica_groups=mesh['dp'=16,'mp'=8] {'mp'}, dimensions={0} | all-to-all | bytes 1441792 | tf_op jit(solution)/shard_map/all_to_all | solution.py:12
  40.8 3.4 %all-to-all-start.3 = ((bf16[8,128,64]{1,2,0:T(8,128)(2,1)}), bf16[8,128,64]{1,2,0:T(8,128)(2,1)S(1)}, u32[]{:S(2)}, u32[]{:S(2)}) async-start(bf16[8,128,64]{1,2,0:T(8,128)(2,1)} %broadcast_in_dim.82), calls=%async_computation.3 | async-start | bytes 262144 | tf_op jit(solution)/shard_map/all_to_all | solution.py:12
  44.9 38.3 %all-gather.4.cloned.1.call-done = bf16[3,1024,1024]{2,1,0:T(8,128)(2,1)} async-done(((bf16[3,64,1024]{2,1,0:T(8,128)(2,1)}), bf16[3,1024,1024]{2,1,0:T(8,128)(2,1)}) %all-gather.4.cloned.1.call-update) | async-done | bytes 6291472 | tf_op jit(solution)/shard_map/all_gather | solution.py:120
  83.1 5.7 %convolution_bitcast_fusion.1 = f32[3,512,1024]{2,1,0:T(8,128)S(1)} fusion(bf16[3,1024,1024]{2,1,0:T(8,128)(2,1)} %all-gather.4.cloned.1.call-done, bf16[512,1024]{1,0:T(8,128)(2,1)S(1)} %copy-done.4, f32[1024]{0:T(1024)S(1)} %bitcast.142, f32[512]{0:T(512)S(1)} %add_rsqrt_fusion.1), kind=kOutput, calls=%fused_computation.45 | convolution fusion | flops 3223322624 | bytes 13637632 | tf_op jit(solution)/shard_map/rc,jcd->jrd/dot_general | solution.py:117
  97.7 3.3 %subtract_convert_fusion.1 = (bf16[512,16,32]{0,2,1:T(8,128)(2,1)S(1)}, bf16[512,16,32]{0,2,1:T(8,128)(2,1)S(1)}, bf16[512,16,32]{0,2,1:T(8,128)(2,1)}, bf16[512,16,32]{0,2,1:T(8,128)(2,1)}) fusion(f32[512,16,64]{0,2,1:T(8,128)S(1)} %bitcast.128, f32[512,32]{0,1:T(8,128)S(1)} %get-tuple-element.84, f32[512,32]{0,1:T(8,128)S(1)} %get-tuple-element.83, ...), kind=kLoop, calls=%fused_computation.64 | loop fusion | flops 4194304 | bytes 6422528 | tf_op jit(solution)/shard_map/convert.3
  104.6 4.4 %all-to-all-start.6 = ((bf16[8,352,64]{1,2,0:T(8,128)(2,1)}), bf16[8,352,64]{1,2,0:T(8,128)(2,1)S(1)}, u32[]{:S(2)}, u32[]{:S(2)}) async-start(bf16[8,352,64]{1,2,0:T(8,128)(2,1)} %broadcast_in_dim.85), calls=%async_computation.6 | async-start | bytes 786432 | tf_op jit(solution)/shard_map/all_to_all | solution.py:12
  115.5 5.7 %copy.40 = bf16[3,512,1024]{1,0,2:T(4,128)(2,1)} copy(bf16[3,512,1024]{2,1,0:T(8,128)(2,1)S(1)} %pad_maximum_fusion) | data formatting | bytes 6291456 | tf_op jit(solution)/shard_map/stack | solution.py:127
  121.2 4.9 %all-to-all-start.1 = ((bf16[3,512,1024]{1,0,2:T(4,128)(2,1)}), bf16[3,512,1024]{1,0,2:T(4,128)(2,1)}, u32[]{:S(2)}, u32[]{:S(2)}) async-start(bf16[3,512,1024]{1,0,2:T(4,128)(2,1)} %copy.40), calls=%async_computation.1 | async-start | bytes 8388608 | tf_op jit(solution)/shard_map/all_to_all | solution.py:126
  126.2 55.5 %all_gather.13 = s32[4096,2]{0,1:T(2,128)S(1)} all-gather(s32[512,2]{0,1:T(2,128)S(1)} %pad_add_fusion), channel_id=1, replica_groups=mesh['dp'=16,'mp'=8] {'mp'}, dimensions={0}, use_global_device_ids=true | all-gather | bytes 36864 | tf_op jit(solution)/shard_map/all_gather | solution.py:30
  184.9 5.8 %all-to-all-start.4 = ((bf16[16,1024,64]{1,2,0:T(8,128)(2,1)}), bf16[16,1024,64]{1,2,0:T(8,128)(2,1)S(1)}, u32[]{:S(2)}, u32[]{:S(2)}) async-start(bf16[16,1024,64]{1,2,0:T(8,128)(2,1)} %broadcast_in_dim.83), calls=%async_computation.4 | async-start | bytes 4194304 | tf_op jit(solution)/shard_map/all_to_all | solution.py:12
  190.7 3.2 %copy.41 = bf16[3,512,1024]{1,2,0:T(8,128)(2,1)S(1)} copy(bf16[3,512,1024]{1,0,2:T(4,128)(2,1)} %all-to-all-done.1) | data formatting | bytes 6291456 | tf_op jit(solution)/shard_map/all_to_all | solution.py:126
  195.7 47.5 %while.10 = (s32[]{:T(128)}, bf16[8,512,2,64]{1,3,2,0:T(8,128)(2,1)}, bf16[8,512,2,64]{1,3,2,0:T(8,128)(2,1)}, s32[8,512]{1,0:T(8,128)S(1)}, bf16[8,512,2,64]{1,...) while((s32[]{:T(128)}, ...), condition=%wide.region_4.5_spmd, body=%wide.region_1.4_spmd.sunk | while | flops 208734208 | bytes 2383009 | solution.py:86
  198.4 3.2 %fusion.92 = bf16[8,512,2,64]{1,3,2,0:T(8,128)(2,1)} fusion(bf16[8,512,2,64]{1,3,2,0:T(8,128)(2,1)} %get-tuple-element.156, s32[]{:T(128)} %get-tuple-element.155, f32[2,512]{1,0:T(2,128)S(1)} %fusion.91, bf16[8,512,2,64]{1,3,2,0:T(8,128)(2,1)} %get-tuple-element.166, f32[2]{0:T(128)S(1)} %get-tuple-element.142, f32[2]{0:T(128)S(1)} %get-tuple-element.143, ...), kind=kOutput, calls=%fused_computation.6.clone.1 | convolution fusion | flops 137954816 | bytes 1054736 | tf_op jit(solution)/shard_map/while/body/eval_jaxpr/hqk,khd->qhd/dot_general | solution.py:81
  204.3 3.2 %fusion.92 = bf16[8,512,2,64]{1,3,2,0:T(8,128)(2,1)} fusion(bf16[8,512,2,64]{1,3,2,0:T(8,128)(2,1)} %get-tuple-element.156, s32[]{:T(128)} %get-tuple-element.155, f32[2,512]{1,0:T(2,128)S(1)} %fusion.91, bf16[8,512,2,64]{1,3,2,0:T(8,128)(2,1)} %get-tuple-element.166, f32[2]{0:T(128)S(1)} %get-tuple-element.142, f32[2]{0:T(128)S(1)} %get-tuple-element.143, ...), kind=kOutput, calls=%fused_computation.6.clone.1 | convolution fusion | flops 137954816 | bytes 1054736 | tf_op jit(solution)/shard_map/while/body/eval_jaxpr/hqk,khd->qhd/dot_general | solution.py:81
  210.2 3.2 %fusion.92 = bf16[8,512,2,64]{1,3,2,0:T(8,128)(2,1)} fusion(bf16[8,512,2,64]{1,3,2,0:T(8,128)(2,1)} %get-tuple-element.156, s32[]{:T(128)} %get-tuple-element.155, f32[2,512]{1,0:T(2,128)S(1)} %fusion.91, bf16[8,512,2,64]{1,3,2,0:T(8,128)(2,1)} %get-tuple-element.166, f32[2]{0:T(128)S(1)} %get-tuple-element.142, f32[2]{0:T(128)S(1)} %get-tuple-element.143, ...), kind=kOutput, calls=%fused_computation.6.clone.1 | convolution fusion | flops 137954816 | bytes 1054736 | tf_op jit(solution)/shard_map/while/body/eval_jaxpr/hqk,khd->qhd/dot_general | solution.py:81
  216.1 3.2 %fusion.92 = bf16[8,512,2,64]{1,3,2,0:T(8,128)(2,1)} fusion(bf16[8,512,2,64]{1,3,2,0:T(8,128)(2,1)} %get-tuple-element.156, s32[]{:T(128)} %get-tuple-element.155, f32[2,512]{1,0:T(2,128)S(1)} %fusion.91, bf16[8,512,2,64]{1,3,2,0:T(8,128)(2,1)} %get-tuple-element.166, f32[2]{0:T(128)S(1)} %get-tuple-element.142, f32[2]{0:T(128)S(1)} %get-tuple-element.143, ...), kind=kOutput, calls=%fused_computation.6.clone.1 | convolution fusion | flops 137954816 | bytes 1054736 | tf_op jit(solution)/shard_map/while/body/eval_jaxpr/hqk,khd->qhd/dot_general | solution.py:81
  222.0 3.2 %fusion.92 = bf16[8,512,2,64]{1,3,2,0:T(8,128)(2,1)} fusion(bf16[8,512,2,64]{1,3,2,0:T(8,128)(2,1)} %get-tuple-element.156, s32[]{:T(128)} %get-tuple-element.155, f32[2,512]{1,0:T(2,128)S(1)} %fusion.91, bf16[8,512,2,64]{1,3,2,0:T(8,128)(2,1)} %get-tuple-element.166, f32[2]{0:T(128)S(1)} %get-tuple-element.142, f32[2]{0:T(128)S(1)} %get-tuple-element.143, ...), kind=kOutput, calls=%fused_computation.6.clone.1 | convolution fusion | flops 137954816 | bytes 1054736 | tf_op jit(solution)/shard_map/while/body/eval_jaxpr/hqk,khd->qhd/dot_general | solution.py:81
  228.0 3.2 %fusion.92 = bf16[8,512,2,64]{1,3,2,0:T(8,128)(2,1)} fusion(bf16[8,512,2,64]{1,3,2,0:T(8,128)(2,1)} %get-tuple-element.156, s32[]{:T(128)} %get-tuple-element.155, f32[2,512]{1,0:T(2,128)S(1)} %fusion.91, bf16[8,512,2,64]{1,3,2,0:T(8,128)(2,1)} %get-tuple-element.166, f32[2]{0:T(128)S(1)} %get-tuple-element.142, f32[2]{0:T(128)S(1)} %get-tuple-element.143, ...), kind=kOutput, calls=%fused_computation.6.clone.1 | convolution fusion | flops 137954816 | bytes 1054736 | tf_op jit(solution)/shard_map/while/body/eval_jaxpr/hqk,khd->qhd/dot_general | solution.py:81
  234.0 3.2 %fusion.92 = bf16[8,512,2,64]{1,3,2,0:T(8,128)(2,1)} fusion(bf16[8,512,2,64]{1,3,2,0:T(8,128)(2,1)} %get-tuple-element.156, s32[]{:T(128)} %get-tuple-element.155, f32[2,512]{1,0:T(2,128)S(1)} %fusion.91, bf16[8,512,2,64]{1,3,2,0:T(8,128)(2,1)} %get-tuple-element.166, f32[2]{0:T(128)S(1)} %get-tuple-element.142, f32[2]{0:T(128)S(1)} %get-tuple-element.143, ...), kind=kOutput, calls=%fused_computation.6.clone.1 | convolution fusion | flops 137954816 | bytes 1054736 | tf_op jit(solution)/shard_map/while/body/eval_jaxpr/hqk,khd->qhd/dot_general | solution.py:81
  239.9 3.2 %fusion.92 = bf16[8,512,2,64]{1,3,2,0:T(8,128)(2,1)} fusion(bf16[8,512,2,64]{1,3,2,0:T(8,128)(2,1)} %get-tuple-element.156, s32[]{:T(128)} %get-tuple-element.155, f32[2,512]{1,0:T(2,128)S(1)} %fusion.91, bf16[8,512,2,64]{1,3,2,0:T(8,128)(2,1)} %get-tuple-element.166, f32[2]{0:T(128)S(1)} %get-tuple-element.142, f32[2]{0:T(128)S(1)} %get-tuple-element.143, ...), kind=kOutput, calls=%fused_computation.6.clone.1 | convolution fusion | flops 137954816 | bytes 1054736 | tf_op jit(solution)/shard_map/while/body/eval_jaxpr/hqk,khd->qhd/dot_general | solution.py:81
  243.2 19.6 %all_to_all.61 = bf16[8,512,128]{1,2,0:T(8,128)(2,1)S(1)} all-to-all(bf16[8,512,128]{1,2,0:T(8,128)(2,1)} %bitcast.134), channel_id=1, replica_groups=mesh['dp'=16,'mp'=8] {'mp'}, dimensions={0} | all-to-all | bytes 2097152 | tf_op jit(solution)/shard_map/all_to_all | solution.py:133
  265.1 12.0 %convolution_bitcast_fusion = f32[2,512,2816]{2,1,0:T(8,128)} fusion(bf16[2,1024,2816]{2,1,0:T(8,128)(2,1)} %all-gather.6.cloned.1.call-done, bf16[512,1024]{1,0:T(8,128)(2,1)} %get-tuple-element.86, f32[1024]{0:T(1024)S(1)} %bitcast.141, f32[512]{0:T(512)S(1)} %add_rsqrt_fusion), kind=kOutput, calls=%fused_computation.32 | convolution fusion | flops 5907677184 | bytes 24123392 | tf_op jit(solution)/shard_map/rc,jcf->jrf/dot_general | solution.py:140
  277.1 10.1 %fusion.52 = bf16[512,1024]{1,0:T(8,128)(2,1)} fusion(bf16[512,1024]{1,0:T(8,128)(2,1)S(1)} %copy-done.3, bf16[2816,1024]{0,1:T(8,128)(2,1)} %all-gather.8.cloned.1.call-done, f32[2,512,2816]{2,1,0:T(8,128)} %convolution_bitcast_fusion), kind=kOutput, calls=%fused_computation.53 | convolution fusion | flops 2963013632 | bytes 19398656 | tf_op jit(solution)/shard_map/dot_general | solution.py:148
  (116 shorter events, 52.9 us)
Async XLA Ops:
  6.5 175.3 %copy-start = (f32[2,16]{1,0:T(2,128)S(1)}, f32[2,16]{1,0:T(2,128)}, u32[]{:S(2)}) copy-start(f32[2,16]{1,0:T(2,128)} %param.16) | copy-start | bytes 388
  6.5 15.8 %copy-start.8 = (bf16[2,64,352]{2,1,0:T(8,128)(2,1)S(1)}, bf16[2,64,352]{2,1,0:T(8,128)(2,1)}, u32[]{:S(2)}) copy-start(bf16[2,64,352]{2,1,0:T(8,128)(2,1)} %param.17) | copy-start | bytes 270340
  6.5 76.6 %all-gather.4.cloned.1.call-start = ((), (), s32[]{:S(2)}) async-start(), calls=%async_computation.7 | async-start | bytes 6684672 | tf_op jit(solution)/shard_map/all_gather | solution.py:120
  22.3 242.8 %all-gather.6.cloned.1.call-start = ((), (), s32[]{:S(2)}) async-start(), calls=%async_computation.8 | async-start | bytes 12255232 | tf_op jit(solution)/shard_map/all_gather | solution.py:143
  38.1 2.1 copy-start.10
  38.1 6.1 %copy-start.12 = (s32[512]{0:T(512)S(1)}, s32[512]{0:T(512)}, u32[]{:S(2)}) copy-start(s32[512]{0:T(512)} %param.21) | copy-start | bytes 6148
  38.1 6.2 %copy-start.4 = (bf16[512,1024]{1,0:T(8,128)(2,1)S(1)}, bf16[512,1024]{1,0:T(8,128)(2,1)}, u32[]{:S(2)}) copy-start(bf16[512,1024]{1,0:T(8,128)(2,1)} %param.12) | copy-start | bytes 3145732
  38.5 6.0 %copy-start.11 = (f32[2,1024]{1,0:T(2,128)S(1)}, f32[2,1024]{1,0:T(2,128)}, u32[]{:S(2)}) copy-start(f32[2,1024]{1,0:T(2,128)} %param.13) | copy-start | bytes 24580
  40.8 63.0 %all-to-all-start.3 = ((bf16[8,128,64]{1,2,0:T(8,128)(2,1)}), bf16[8,128,64]{1,2,0:T(8,128)(2,1)S(1)}, u32[]{:S(2)}, u32[]{:S(2)}) async-start(bf16[8,128,64]{1,2,0:T(8,128)(2,1)} %broadcast_in_dim.82), calls=%async_computation.3 | async-start | bytes 262144 | tf_op jit(solution)/shard_map/all_to_all | solution.py:12
  88.9 3.8 %copy-start.2 = (f32[3,512,1024]{2,1,0:T(8,128)}, f32[3,512,1024]{2,1,0:T(8,128)S(1)}, u32[]{:S(2)}) copy-start(f32[3,512,1024]{2,1,0:T(8,128)S(1)} %convolution_bitcast_fusion.1) | copy-start | bytes 18874372
  101.0 2.8 copy-start.9
  103.8 0.8 copy-start.6
  104.6 16.6 %all-to-all-start.6 = ((bf16[8,352,64]{1,2,0:T(8,128)(2,1)}), bf16[8,352,64]{1,2,0:T(8,128)(2,1)S(1)}, u32[]{:S(2)}, u32[]{:S(2)}) async-start(bf16[8,352,64]{1,2,0:T(8,128)(2,1)} %broadcast_in_dim.85), calls=%async_computation.6 | async-start | bytes 786432 | tf_op jit(solution)/shard_map/all_to_all | solution.py:12
  121.2 5.0 %copy-start.13 = (s32[512]{0:T(512)S(1)}, s32[512]{0:T(512)}, u32[]{:S(2)}) copy-start(s32[512]{0:T(512)} %param.20) | copy-start | bytes 6148
  121.2 5.0 %copy-start.14 = (s32[512]{0:T(512)S(1)}, s32[512]{0:T(512)}, u32[]{:S(2)}) copy-start(s32[512]{0:T(512)} %param.19) | copy-start | bytes 6148
  121.2 60.8 %copy-start.7 = (bf16[8,128,64]{1,2,0:T(8,128)(2,1)S(1)}, bf16[8,128,64]{1,2,0:T(8,128)(2,1)}, u32[]{:S(2)}) copy-start(bf16[8,128,64]{1,2,0:T(8,128)(2,1)} %copy-done.6) | copy-start | bytes 393220
  121.2 62.1 %all-to-all-start.1 = ((bf16[3,512,1024]{1,0,2:T(4,128)(2,1)}), bf16[3,512,1024]{1,0,2:T(4,128)(2,1)}, u32[]{:S(2)}, u32[]{:S(2)}) async-start(bf16[3,512,1024]{1,0,2:T(4,128)(2,1)} %copy.40), calls=%async_computation.1 | async-start | bytes 8388608 | tf_op jit(solution)/shard_map/all_to_all | solution.py:126
  126.1 151.0 %all-gather.8.cloned.1.call-start = ((), (), s32[]{:S(2)}) async-start(), calls=%async_computation.9 | async-start | bytes 6127616 | tf_op jit(solution)/shard_map/all_gather | solution.py:150
  184.9 58.3 %all-to-all-start.4 = ((bf16[16,1024,64]{1,2,0:T(8,128)(2,1)}), bf16[16,1024,64]{1,2,0:T(8,128)(2,1)S(1)}, u32[]{:S(2)}, u32[]{:S(2)}) async-start(bf16[16,1024,64]{1,2,0:T(8,128)(2,1)} %broadcast_in_dim.83), calls=%async_computation.4 | async-start | bytes 4194304 | tf_op jit(solution)/shard_map/all_to_all | solution.py:12
  243.2 19.6 %copy-start.5 = (bf16[512,1024]{1,0:T(8,128)(2,1)S(1)}, bf16[512,1024]{1,0:T(8,128)(2,1)}, u32[]{:S(2)}) copy-start(bf16[512,1024]{1,0:T(8,128)(2,1)} %param.12) | copy-start | bytes 3145732
  265.1 12.0 %copy-start.3 = (bf16[512,1024]{1,0:T(8,128)(2,1)S(1)}, bf16[512,1024]{1,0:T(8,128)(2,1)}, u32[]{:S(2)}) copy-start(bf16[512,1024]{1,0:T(8,128)(2,1)} %get-tuple-element.86) | copy-start | bytes 3145732
  277.1 10.1 %copy-start.1 = (f32[2,16]{1,0:T(2,128)S(1)}, f32[2,16]{1,0:T(2,128)}, u32[]{:S(2)}) copy-start(f32[2,16]{1,0:T(2,128)} %param.16) | copy-start | bytes 388
Sparse Core Ops, SparseCore 0:
  22.4 60.6 all-gather.3
  85.3 84.4 all-gather.5
  183.4 74.9 all-gather.7
where the time goes:
time: 295 us; the launch traced here: 294 us
  blocking collectives  105 us (36%)
  matrix products  73.9 us (25%)
  waiting for transfers between devices  38.4 us (13%)
  local copies, waits for them, and re-layouts  33.5 us (11%)
  starting transfers between devices  18.6 us (6%)
  between operations  13.4 us (5%)
  other arithmetic  11.1 us (4%)
    all_gather x1, blocking collectives, rows_first(): whole = lax.all_gather(both, axis, axis=0, tiled=True)  55.5 us
    all_gather x1, waiting for transfers between devices, local(): lax.all_gather(wide_columns, 'dp', axis=1, tiled=True)  38.3 us
    all_to_all x2, blocking collectives, sent_to_all(): return lax.all_to_all(copies, axis, split_axis=0, concat_axis=0, tiled=True)  29.6 us
    dot_general x8, matrix products, one_sequence(): jnp.einsum('hqk,khd->qhd', weights, vs, preferred_element_type=jnp.float32)  25.7 us
    all_to_all x1, blocking collectives, local(): lax.all_to_all(attended, 'mp', split_axis=0, concat_axis=1, tiled=True)  19.6 us
    sub x8, matrix products, one_sequence(): expo = jnp.exp(scores - top)  18 us
    all_to_all x3, starting transfers between devices, sent_to_all(): return lax.all_to_all(copies, axis, split_axis=0, concat_axis=0, tiled=True)  13.6 us
    dot_general x1, matrix products, local(): jnp.einsum('rc,jcf->jrf', columns, lax.all_gather(ffn_columns, 'dp', axis...  12 us
  transfers between devices with their start and end apart: 7, of which 1 were waited for; matrix products, arithmetic and copies ran while one was open for 36% of the time, Pallas kernels for 0%

commit v1 on v0

--- a/solution.py
+++ b/solution.py
@@ -117,7 +117,7 @@
     projected = jnp.einsum(
         "rc,jcd->jrd",
         columns,
-        lax.all_gather(wide_columns, "dp", axis=1, tiled=True),
+        jnp.concatenate(lax.all_gather(wide_columns, "dp"), axis=1),
         preferred_element_type=jnp.float32,
     )
     queries = rotated(projected[0], time_ids)

time: 295 us -> 297 us (level)
  local copies, waits for them, and re-layouts: 33.5 us -> 37.5 us
    reshape x0 -> x1, local copies, waits for them, and re-layouts: none -> 3.49 us  [local(): jnp.concatenate(lax.all_gather(wide_columns, 'dp'), axis=1)]
where the time goes in v1:
time: 297 us; the launch traced here: 295 us
  blocking collectives  105 us (35%)
  matrix products  71.7 us (24%)
  waiting for transfers between devices  38.4 us (13%)
  local copies, waits for them, and re-layouts  37.5 us (13%)
  starting transfers between devices  18.4 us (6%)
  between operations  13.4 us (5%)
  other arithmetic  11.1 us (4%)
    all_gather x1, blocking collectives, rows_first(): whole = lax.all_gather(both, axis, axis=0, tiled=True)  55.5 us
    all_gather x1, waiting for transfers between devices, local(): lax.all_gather(wide_columns, 'dp')  38.3 us
    all_to_all x2, blocking collectives, sent_to_all(): return lax.all_to_all(copies, axis, split_axis=0, concat_axis=0, tiled=True)  29.6 us
    dot_general x8, matrix products, one_sequence(): jnp.einsum('hqk,khd->qhd', weights, vs, preferred_element_type=jnp.float32)  25.7 us
    all_to_all x1, blocking collectives, local(): lax.all_to_all(attended, 'mp', split_axis=0, concat_axis=1, tiled=True)  19.6 us
    sub x8, matrix products, one_sequence(): expo = jnp.exp(scores - top)  18 us
    all_to_all x3, starting transfers between devices, sent_to_all(): return lax.all_to_all(copies, axis, split_axis=0, concat_axis=0, tiled=True)  13.4 us
    dot_general x1, matrix products, local(): jnp.einsum('rc,jcf->jrf', columns, lax.all_gather(ffn_columns, 'dp', axis...  12 us
  transfers between devices with their start and end apart: 7, of which 1 were waited for; matrix products, arithmetic and copies ran while one was open for 36% of the time, Pallas kernels for 0%

profile of v1, /device:TPU:2, one launch (start us, length us, event | category | flops | bytes accessed | tf_op | source)
XLA Modules:
  0.0 295.4 jit_solution(8293301190600336016)
XLA Ops:
  7.5 14.0 %all_to_all.59 = bf16[8,3,64,128]{3,2,1,0:T(8,128)(2,1)S(1)} all-to-all(bf16[8,3,64,128]{3,2,1,0:T(8,128)(2,1)S(1)} %broadcast_in_dim.81), channel_id=1, replica_groups=mesh['dp'=16,'mp'=8] {'mp'}, dimensions={0} | all-to-all | bytes 786432 | tf_op jit(solution)/shard_map/all_to_all | solution.py:12
  22.8 15.6 %all_to_all.60 = bf16[8,2,64,352]{3,2,1,0:T(8,128)(2,1)S(1)} all-to-all(bf16[8,2,64,352]{3,2,1,0:T(8,128)(2,1)S(1)} %broadcast_in_dim.84), channel_id=1, replica_groups=mesh['dp'=16,'mp'=8] {'mp'}, dimensions={0} | all-to-all | bytes 1441792 | tf_op jit(solution)/shard_map/all_to_all | solution.py:12
  41.2 3.4 %all-to-all-start.3 = ((bf16[8,128,64]{1,2,0:T(8,128)(2,1)}), bf16[8,128,64]{1,2,0:T(8,128)(2,1)S(1)}, u32[]{:S(2)}, u32[]{:S(2)}) async-start(bf16[8,128,64]{1,2,0:T(8,128)(2,1)} %broadcast_in_dim.82), calls=%async_computation.3 | async-start | bytes 262144 | tf_op jit(solution)/shard_map/all_to_all | solution.py:12
  45.2 38.3 %all-gather.4.cloned.1.call-done = bf16[16,3,64,1024]{3,2,1,0:T(8,128)(2,1)} async-done(((bf16[1,3,64,1024]{3,2,1,0:T(8,128)(2,1)}), bf16[16,3,64,1024]{3,2,1,0:T(8,128)(2,1)}) %all-gather.4.cloned.1.call-update) | async-done | bytes 6291472 | tf_op jit(solution)/shard_map/all_gather | solution.py:120
  83.5 3.5 %copy.47 = bf16[3,16,64,1024]{3,2,1,0:T(8,128)(2,1)S(1)} copy(bf16[3,16,64,1024]{3,2,0,1:T(8,128)(2,1)} %bitcast.129) | data formatting | bytes 12582912 | tf_op jit(solution)/shard_map/reshape | solution.py:120
  87.0 3.6 %convolution_bitcast_fusion.1 = f32[3,512,1024]{2,1,0:T(8,128)S(1)} fusion(bf16[3,1024,1024]{2,1,0:T(8,128)(2,1)S(1)} %bitcast.130, bf16[512,1024]{1,0:T(8,128)(2,1)S(1)} %copy-done.4, f32[1024]{0:T(1024)S(1)} %bitcast.144, f32[512]{0:T(512)S(1)} %add_rsqrt_fusion.1), kind=kOutput, calls=%fused_computation.45 | convolution fusion | flops 3223322624 | bytes 13637632 | tf_op jit(solution)/shard_map/rc,jcd->jrd/dot_general | solution.py:117
  99.6 3.3 %subtract_convert_fusion.1 = (bf16[512,16,32]{0,2,1:T(8,128)(2,1)S(1)}, bf16[512,16,32]{0,2,1:T(8,128)(2,1)S(1)}, bf16[512,16,32]{0,2,1:T(8,128)(2,1)}, bf16[512,16,32]{0,2,1:T(8,128)(2,1)}) fusion(f32[512,16,64]{0,2,1:T(8,128)S(1)} %bitcast.127, f32[512,32]{0,1:T(8,128)S(1)} %get-tuple-element.84, f32[512,32]{0,1:T(8,128)S(1)} %get-tuple-element.83, ...), kind=kLoop, calls=%fused_computation.64 | loop fusion | flops 4194304 | bytes 6422528 | tf_op jit(solution)/shard_map/convert.3
  106.4 4.4 %all-to-all-start.6 = ((bf16[8,352,64]{1,2,0:T(8,128)(2,1)}), bf16[8,352,64]{1,2,0:T(8,128)(2,1)S(1)}, u32[]{:S(2)}, u32[]{:S(2)}) async-start(bf16[8,352,64]{1,2,0:T(8,128)(2,1)} %broadcast_in_dim.85), calls=%async_computation.6 | async-start | bytes 786432 | tf_op jit(solution)/shard_map/all_to_all | solution.py:12
  117.3 5.7 %copy.52 = bf16[3,512,1024]{1,0,2:T(4,128)(2,1)} copy(bf16[3,512,1024]{2,1,0:T(8,128)(2,1)S(1)} %pad_maximum_fusion) | data formatting | bytes 6291456 | tf_op jit(solution)/shard_map/stack | solution.py:127
  123.0 4.9 %all-to-all-start.1 = ((bf16[3,512,1024]{1,0,2:T(4,128)(2,1)}), bf16[3,512,1024]{1,0,2:T(4,128)(2,1)}, u32[]{:S(2)}, u32[]{:S(2)}) async-start(bf16[3,512,1024]{1,0,2:T(4,128)(2,1)} %copy.52), calls=%async_computation.1 | async-start | bytes 8388608 | tf_op jit(solution)/shard_map/all_to_all | solution.py:126
  128.1 55.5 %all_gather.13 = s32[4096,2]{0,1:T(2,128)S(1)} all-gather(s32[512,2]{0,1:T(2,128)S(1)} %pad_add_fusion), channel_id=1, replica_groups=mesh['dp'=16,'mp'=8] {'mp'}, dimensions={0}, use_global_device_ids=true | all-gather | bytes 36864 | tf_op jit(solution)/shard_map/all_gather | solution.py:30
  186.7 5.6 %all-to-all-start.4 = ((bf16[16,1024,64]{1,2,0:T(8,128)(2,1)}), bf16[16,1024,64]{1,2,0:T(8,128)(2,1)S(1)}, u32[]{:S(2)}, u32[]{:S(2)}) async-start(bf16[16,1024,64]{1,2,0:T(8,128)(2,1)} %broadcast_in_dim.83), calls=%async_computation.4 | async-start | bytes 4194304 | tf_op jit(solution)/shard_map/all_to_all | solution.py:12
  197.3 47.4 %while.10 = (s32[]{:T(128)}, bf16[8,512,2,64]{1,3,2,0:T(8,128)(2,1)}, bf16[8,512,2,64]{1,3,2,0:T(8,128)(2,1)}, s32[8,512]{1,0:T(8,128)S(1)}, bf16[8,512,2,64]{1,...) while((s32[]{:T(128)}, ...), condition=%wide.region_4.5_spmd, body=%wide.region_1.4_spmd.sunk | while | flops 208734208 | bytes 2383009 | solution.py:86
  200.0 3.2 %fusion.91 = bf16[8,512,2,64]{1,3,2,0:T(8,128)(2,1)} fusion(bf16[8,512,2,64]{1,3,2,0:T(8,128)(2,1)} %get-tuple-element.156, s32[]{:T(128)} %get-tuple-element.155, f32[2,512]{1,0:T(2,128)S(1)} %fusion.90, bf16[8,512,2,64]{1,3,2,0:T(8,128)(2,1)} %get-tuple-element.166, f32[2]{0:T(128)S(1)} %get-tuple-element.142, f32[2]{0:T(128)S(1)} %get-tuple-element.143, ...), kind=kOutput, calls=%fused_computation.6.clone.1 | convolution fusion | flops 137954816 | bytes 1054736 | tf_op jit(solution)/shard_map/while/body/eval_jaxpr/hqk,khd->qhd/dot_general | solution.py:81
  205.9 3.2 %fusion.91 = bf16[8,512,2,64]{1,3,2,0:T(8,128)(2,1)} fusion(bf16[8,512,2,64]{1,3,2,0:T(8,128)(2,1)} %get-tuple-element.156, s32[]{:T(128)} %get-tuple-element.155, f32[2,512]{1,0:T(2,128)S(1)} %fusion.90, bf16[8,512,2,64]{1,3,2,0:T(8,128)(2,1)} %get-tuple-element.166, f32[2]{0:T(128)S(1)} %get-tuple-element.142, f32[2]{0:T(128)S(1)} %get-tuple-element.143, ...), kind=kOutput, calls=%fused_computation.6.clone.1 | convolution fusion | flops 137954816 | bytes 1054736 | tf_op jit(solution)/shard_map/while/body/eval_jaxpr/hqk,khd->qhd/dot_general | solution.py:81
  211.8 3.2 %fusion.91 = bf16[8,512,2,64]{1,3,2,0:T(8,128)(2,1)} fusion(bf16[8,512,2,64]{1,3,2,0:T(8,128)(2,1)} %get-tuple-element.156, s32[]{:T(128)} %get-tuple-element.155, f32[2,512]{1,0:T(2,128)S(1)} %fusion.90, bf16[8,512,2,64]{1,3,2,0:T(8,128)(2,1)} %get-tuple-element.166, f32[2]{0:T(128)S(1)} %get-tuple-element.142, f32[2]{0:T(128)S(1)} %get-tuple-element.143, ...), kind=kOutput, calls=%fused_computation.6.clone.1 | convolution fusion | flops 137954816 | bytes 1054736 | tf_op jit(solution)/shard_map/while/body/eval_jaxpr/hqk,khd->qhd/dot_general | solution.py:81
  217.7 3.2 %fusion.91 = bf16[8,512,2,64]{1,3,2,0:T(8,128)(2,1)} fusion(bf16[8,512,2,64]{1,3,2,0:T(8,128)(2,1)} %get-tuple-element.156, s32[]{:T(128)} %get-tuple-element.155, f32[2,512]{1,0:T(2,128)S(1)} %fusion.90, bf16[8,512,2,64]{1,3,2,0:T(8,128)(2,1)} %get-tuple-element.166, f32[2]{0:T(128)S(1)} %get-tuple-element.142, f32[2]{0:T(128)S(1)} %get-tuple-element.143, ...), kind=kOutput, calls=%fused_computation.6.clone.1 | convolution fusion | flops 137954816 | bytes 1054736 | tf_op jit(solution)/shard_map/while/body/eval_jaxpr/hqk,khd->qhd/dot_general | solution.py:81
  223.6 3.2 %fusion.91 = bf16[8,512,2,64]{1,3,2,0:T(8,128)(2,1)} fusion(bf16[8,512,2,64]{1,3,2,0:T(8,128)(2,1)} %get-tuple-element.156, s32[]{:T(128)} %get-tuple-element.155, f32[2,512]{1,0:T(2,128)S(1)} %fusion.90, bf16[8,512,2,64]{1,3,2,0:T(8,128)(2,1)} %get-tuple-element.166, f32[2]{0:T(128)S(1)} %get-tuple-element.142, f32[2]{0:T(128)S(1)} %get-tuple-element.143, ...), kind=kOutput, calls=%fused_computation.6.clone.1 | convolution fusion | flops 137954816 | bytes 1054736 | tf_op jit(solution)/shard_map/while/body/eval_jaxpr/hqk,khd->qhd/dot_general | solution.py:81
  229.6 3.2 %fusion.91 = bf16[8,512,2,64]{1,3,2,0:T(8,128)(2,1)} fusion(bf16[8,512,2,64]{1,3,2,0:T(8,128)(2,1)} %get-tuple-element.156, s32[]{:T(128)} %get-tuple-element.155, f32[2,512]{1,0:T(2,128)S(1)} %fusion.90, bf16[8,512,2,64]{1,3,2,0:T(8,128)(2,1)} %get-tuple-element.166, f32[2]{0:T(128)S(1)} %get-tuple-element.142, f32[2]{0:T(128)S(1)} %get-tuple-element.143, ...), kind=kOutput, calls=%fused_computation.6.clone.1 | convolution fusion | flops 137954816 | bytes 1054736 | tf_op jit(solution)/shard_map/while/body/eval_jaxpr/hqk,khd->qhd/dot_general | solution.py:81
  235.6 3.2 %fusion.91 = bf16[8,512,2,64]{1,3,2,0:T(8,128)(2,1)} fusion(bf16[8,512,2,64]{1,3,2,0:T(8,128)(2,1)} %get-tuple-element.156, s32[]{:T(128)} %get-tuple-element.155, f32[2,512]{1,0:T(2,128)S(1)} %fusion.90, bf16[8,512,2,64]{1,3,2,0:T(8,128)(2,1)} %get-tuple-element.166, f32[2]{0:T(128)S(1)} %get-tuple-element.142, f32[2]{0:T(128)S(1)} %get-tuple-element.143, ...), kind=kOutput, calls=%fused_computation.6.clone.1 | convolution fusion | flops 137954816 | bytes 1054736 | tf_op jit(solution)/shard_map/while/body/eval_jaxpr/hqk,khd->qhd/dot_general | solution.py:81
  241.5 3.2 %fusion.91 = bf16[8,512,2,64]{1,3,2,0:T(8,128)(2,1)} fusion(bf16[8,512,2,64]{1,3,2,0:T(8,128)(2,1)} %get-tuple-element.156, s32[]{:T(128)} %get-tuple-element.155, f32[2,512]{1,0:T(2,128)S(1)} %fusion.90, bf16[8,512,2,64]{1,3,2,0:T(8,128)(2,1)} %get-tuple-element.166, f32[2]{0:T(128)S(1)} %get-tuple-element.142, f32[2]{0:T(128)S(1)} %get-tuple-element.143, ...), kind=kOutput, calls=%fused_computation.6.clone.1 | convolution fusion | flops 137954816 | bytes 1054736 | tf_op jit(solution)/shard_map/while/body/eval_jaxpr/hqk,khd->qhd/dot_general | solution.py:81
  244.8 19.6 %all_to_all.61 = bf16[8,512,128]{1,2,0:T(8,128)(2,1)S(1)} all-to-all(bf16[8,512,128]{1,2,0:T(8,128)(2,1)} %bitcast.136), channel_id=1, replica_groups=mesh['dp'=16,'mp'=8] {'mp'}, dimensions={0} | all-to-all | bytes 2097152 | tf_op jit(solution)/shard_map/all_to_all | solution.py:133
  266.7 12.0 %convolution_bitcast_fusion = f32[2,512,2816]{2,1,0:T(8,128)} fusion(bf16[2,1024,2816]{2,1,0:T(8,128)(2,1)} %all-gather.6.cloned.1.call-done, bf16[512,1024]{1,0:T(8,128)(2,1)} %get-tuple-element.86, f32[1024]{0:T(1024)S(1)} %bitcast.143, f32[512]{0:T(512)S(1)} %add_rsqrt_fusion), kind=kOutput, calls=%fused_computation.32 | convolution fusion | flops 5907677184 | bytes 24123392 | tf_op jit(solution)/shard_map/rc,jcf->jrf/dot_general | solution.py:140
  278.7 10.1 %fusion.52 = bf16[512,1024]{1,0:T(8,128)(2,1)} fusion(bf16[512,1024]{1,0:T(8,128)(2,1)S(1)} %copy-done.3, bf16[2816,1024]{0,1:T(8,128)(2,1)} %all-gather.8.cloned.1.call-done, f32[2,512,2816]{2,1,0:T(8,128)} %convolution_bitcast_fusion), kind=kOutput, calls=%fused_computation.53 | convolution fusion | flops 2963013632 | bytes 19398656 | tf_op jit(solution)/shard_map/dot_general | solution.py:148
  (118 shorter events, 56.6 us)
Async XLA Ops:
  6.5 177.2 %copy-start = (f32[2,16]{1,0:T(2,128)S(1)}, f32[2,16]{1,0:T(2,128)}, u32[]{:S(2)}) copy-start(f32[2,16]{1,0:T(2,128)} %param.16) | copy-start | bytes 388
  6.5 16.2 %copy-start.8 = (bf16[2,64,352]{2,1,0:T(8,128)(2,1)S(1)}, bf16[2,64,352]{2,1,0:T(8,128)(2,1)}, u32[]{:S(2)}) copy-start(bf16[2,64,352]{2,1,0:T(8,128)(2,1)} %param.17) | copy-start | bytes 270340
  6.5 77.0 %all-gather.4.cloned.1.call-start = ((), (), s32[]{:S(2)}) async-start(), calls=%async_computation.7 | async-start | bytes 6684672 | tf_op jit(solution)/shard_map/all_gather | solution.py:120
  22.7 244.0 %all-gather.6.cloned.1.call-start = ((), (), s32[]{:S(2)}) async-start(), calls=%async_computation.8 | async-start | bytes 12255232 | tf_op jit(solution)/shard_map/all_gather | solution.py:143
  38.4 2.1 copy-start.10
  38.4 6.1 %copy-start.12 = (s32[512]{0:T(512)S(1)}, s32[512]{0:T(512)}, u32[]{:S(2)}) copy-start(s32[512]{0:T(512)} %param.21) | copy-start | bytes 6148
  38.4 6.2 %copy-start.4 = (bf16[512,1024]{1,0:T(8,128)(2,1)S(1)}, bf16[512,1024]{1,0:T(8,128)(2,1)}, u32[]{:S(2)}) copy-start(bf16[512,1024]{1,0:T(8,128)(2,1)} %param.12) | copy-start | bytes 3145732
  38.9 6.0 %copy-start.11 = (f32[2,1024]{1,0:T(2,128)S(1)}, f32[2,1024]{1,0:T(2,128)}, u32[]{:S(2)}) copy-start(f32[2,1024]{1,0:T(2,128)} %param.13) | copy-start | bytes 24580
  41.2 64.5 %all-to-all-start.3 = ((bf16[8,128,64]{1,2,0:T(8,128)(2,1)}), bf16[8,128,64]{1,2,0:T(8,128)(2,1)S(1)}, u32[]{:S(2)}, u32[]{:S(2)}) async-start(bf16[8,128,64]{1,2,0:T(8,128)(2,1)} %broadcast_in_dim.82), calls=%async_computation.3 | async-start | bytes 262144 | tf_op jit(solution)/shard_map/all_to_all | solution.py:12
  90.6 3.9 %copy-start.2 = (f32[3,512,1024]{2,1,0:T(8,128)}, f32[3,512,1024]{2,1,0:T(8,128)S(1)}, u32[]{:S(2)}) copy-start(f32[3,512,1024]{2,1,0:T(8,128)S(1)} %convolution_bitcast_fusion.1) | copy-start | bytes 18874372
  102.9 2.8 copy-start.9
  105.6 0.8 copy-start.6
  106.4 16.6 %all-to-all-start.6 = ((bf16[8,352,64]{1,2,0:T(8,128)(2,1)}), bf16[8,352,64]{1,2,0:T(8,128)(2,1)S(1)}, u32[]{:S(2)}, u32[]{:S(2)}) async-start(bf16[8,352,64]{1,2,0:T(8,128)(2,1)} %broadcast_in_dim.85), calls=%async_computation.6 | async-start | bytes 786432 | tf_op jit(solution)/shard_map/all_to_all | solution.py:12
  123.0 5.0 %copy-start.13 = (s32[512]{0:T(512)S(1)}, s32[512]{0:T(512)}, u32[]{:S(2)}) copy-start(s32[512]{0:T(512)} %param.20) | copy-start | bytes 6148
  123.0 5.0 %copy-start.14 = (s32[512]{0:T(512)S(1)}, s32[512]{0:T(512)}, u32[]{:S(2)}) copy-start(s32[512]{0:T(512)} %param.19) | copy-start | bytes 6148
  123.0 60.8 %copy-start.7 = (bf16[8,128,64]{1,2,0:T(8,128)(2,1)S(1)}, bf16[8,128,64]{1,2,0:T(8,128)(2,1)}, u32[]{:S(2)}) copy-start(bf16[8,128,64]{1,2,0:T(8,128)(2,1)} %copy-done.6) | copy-start | bytes 393220
  123.0 62.1 %all-to-all-start.1 = ((bf16[3,512,1024]{1,0,2:T(4,128)(2,1)}), bf16[3,512,1024]{1,0,2:T(4,128)(2,1)}, u32[]{:S(2)}, u32[]{:S(2)}) async-start(bf16[3,512,1024]{1,0,2:T(4,128)(2,1)} %copy.52), calls=%async_computation.1 | async-start | bytes 8388608 | tf_op jit(solution)/shard_map/all_to_all | solution.py:126
  128.0 150.7 %all-gather.8.cloned.1.call-start = ((), (), s32[]{:S(2)}) async-start(), calls=%async_computation.9 | async-start | bytes 6127616 | tf_op jit(solution)/shard_map/all_gather | solution.py:150
  186.7 58.0 %all-to-all-start.4 = ((bf16[16,1024,64]{1,2,0:T(8,128)(2,1)}), bf16[16,1024,64]{1,2,0:T(8,128)(2,1)S(1)}, u32[]{:S(2)}, u32[]{:S(2)}) async-start(bf16[16,1024,64]{1,2,0:T(8,128)(2,1)} %broadcast_in_dim.83), calls=%async_computation.4 | async-start | bytes 4194304 | tf_op jit(solution)/shard_map/all_to_all | solution.py:12
  244.8 19.6 %copy-start.5 = (bf16[512,1024]{1,0:T(8,128)(2,1)S(1)}, bf16[512,1024]{1,0:T(8,128)(2,1)}, u32[]{:S(2)}) copy-start(bf16[512,1024]{1,0:T(8,128)(2,1)} %param.12) | copy-start | bytes 3145732
  266.7 12.0 %copy-start.3 = (bf16[512,1024]{1,0:T(8,128)(2,1)S(1)}, bf16[512,1024]{1,0:T(8,128)(2,1)}, u32[]{:S(2)}) copy-start(bf16[512,1024]{1,0:T(8,128)(2,1)} %get-tuple-element.86) | copy-start | bytes 3145732
  278.7 10.1 %copy-start.1 = (f32[2,16]{1,0:T(2,128)S(1)}, f32[2,16]{1,0:T(2,128)}, u32[]{:S(2)}) copy-start(f32[2,16]{1,0:T(2,128)} %param.16) | copy-start | bytes 388
Sparse Core Ops, SparseCore 0:
  22.8 60.6 all-gather.3
  85.6 84.4 all-gather.5
  185.3 74.6 all-gather.7
